TPU v7x, 32 devices: a whole 2x2x4 slice. The times are simulated.
32 devices in a mesh: dp: 8 (over z, x), mp: 4 (over y, core).
Axes of the slice: x: 2, y: 2, z: 4, core: 2. Of those that a mesh axis runs over, the one named last changes fastest.
Arguments:
- acts: bfloat16 [1, 16384, 4096], P(None, 'dp'), may hold values from -64 to 64
- out_grads: bfloat16 [1, 16384, 4096], P(None, 'dp', 'mp'), may hold values from -80 to 80
- clip_bound: float32 [1], replicated, may hold values from 163840 to 491520
- noise: float32 [1, 4096, 4096], P(None, 'dp', 'mp'), may hold values from -6 to 6
Outputs:
- update: float32 [1, 4096, 4096], P(None, 'dp', 'mp')
All inputs are finite; a program needn't handle non-finite values.
Results may differ from a plain program's by a relative error of at most 0.0017.
Values may be sent and summed in bfloat16 or wider, within the bound.
A program may use at most 128 MiB of HBM per device.

v0:
```python
import math
import jax
import jax.numpy as jnp
from jax import lax
from jax.sharding import PartitionSpec as P

SEQ = 512


def ghost_partial(act_block, grad_block, examples):
    act_seq = act_block.reshape(examples, SEQ, act_block.shape[1])
    grad_seq = grad_block.reshape(examples, SEQ, grad_block.shape[1])
    gram_act = jnp.einsum("etd,esd->ets", act_seq, act_seq, preferred_element_type=jnp.float32)
    gram_grad = jnp.einsum("etd,esd->ets", grad_seq, grad_seq, preferred_element_type=jnp.float32)
    return jnp.sum(gram_act * gram_grad, axis=(1, 2))


def scale_grads(grad_block, norm_sq, bound, examples):
    clip = jnp.minimum(1.0, bound / jnp.sqrt(norm_sq + 1e-06))
    factor = clip / bound
    grad_seq = grad_block.reshape(examples, SEQ, grad_block.shape[1]).astype(jnp.float32)
    scaled = (grad_seq * factor[:, None, None]).astype(jnp.bfloat16)
    return scaled.reshape(grad_block.shape)


def on_device(acts, out_grads, clip_bound, noise):
    examples = acts.shape[1] // SEQ
    model_width = acts.shape[2]
    batch_total = examples * lax.axis_size("dp")
    out_factor = model_width / math.sqrt(batch_total)
    act_block = acts[0]
    norm_sq = lax.psum(ghost_partial(act_block, out_grads[0], examples), "mp")
    scaled = scale_grads(out_grads[0], norm_sq, clip_bound[0], examples)

    def term_rows(begin_row, row_count, act_block=act_block, scaled=scaled):
        return lax.dot_general(
            act_block, scaled, (((0,), (0,)), ((), ())), preferred_element_type=jnp.float32
        )

    summed = lax.psum_scatter(
        term_rows(jnp.int32(0), model_width // lax.axis_size("dp") * lax.axis_size("dp")),
        "dp",
        scatter_dimension=0,
        tiled=True,
    )
    updates = [summed * out_factor + noise[0]]
    return jnp.stack(updates)


def solution(mesh):
    placed = (P(None, "dp", None), P(None, "dp", "mp"), P(), P(None, "dp", "mp"))
    return jax.shard_map(
        on_device, mesh=mesh, in_specs=placed, out_specs=P(None, "dp", "mp"), check_vma=False
    )
```

profile of v0, /device:TPU:0, one launch (start us, length us, event | category | flops | bytes accessed | tf_op | source)
XLA Modules:
  0.0 358.5 jit_solution(12628637458226172755)
XLA Ops:
  6.5 0.0 reduce-scatter.2.cloned.1.call-start
  6.5 7.8 %fusion.9 = f32[4,512,512]{2,1,0:T(8,128)} fusion(bf16[4,512,1024]{2,1,0:T(8,128)(2,1)} %bitcast.29), kind=kOutput, calls=%fused_computation.11 | convolution fusion | flops 2147483648 | bytes 8388608 | tf_op jit(solution)/shard_map/etd,esd->ets/dot_general | solution.py:14
  14.3 16.9 %multiply_reduce_fusion = f32[4]{0:T(128)S(1)} fusion(f32[4,512,512]{2,1,0:T(8,128)} %fusion.9, bf16[4,512,4096]{2,1,0:T(8,128)(2,1)} %bitcast.28), kind=kOutput, calls=%fused_computation.6 | convolution fusion | flops 8592031744 | bytes 20971536 | tf_op jit(solution)/shard_map/etd,esd->ets/dot_general | solution.py:13
  31.2 8.6 %psum.7 = f32[4]{0:T(128)S(1)} all-reduce(f32[4]{0:T(128)S(1)} %multiply_reduce_fusion), channel_id=1, replica_groups=mesh['dp'=8,'mp'=4] {'mp'}, use_global_device_ids=true, to_apply=%region_1.0 | all-reduce | flops 4 | bytes 32 | tf_op jit(solution)/shard_map/psum | solution.py:32
  40.4 0.1 broadcast_bitcast_fusion
  40.5 24.2 %fusion.2 = f32[4096,1024]{0,1:T(8,128)} fusion(bf16[1,2048,4096]{2,1,0:T(8,128)(2,1)} %param.4, bf16[1,2048,1024]{2,1,0:T(8,128)(2,1)} %param.5, f32[2048]{0:T(1024)S(1)} %bitcast.27), kind=kOutput, calls=%fused_computation.2 | convolution fusion | flops 17186160640 | bytes 37756928 | tf_op jit(solution)/shard_map/dot_general | solution.py:36
  64.7 0.0 reduce-scatter.2.cloned.1.call-update
  64.7 1.9 copy.5
  66.7 278.7 %reduce-scatter.2.cloned.1.call-done = f32[512,1024]{0,1:T(8,128)} async-done(((f32[4096,1024]{0,1:T(8,128)}), f32[512,1024]{0,1:T(8,128)}) %reduce-scatter.2.cloned.1.call-update) | async-done | bytes 2097168 | tf_op jit(solution)/shard_map/reduce_scatter | solution.py:40
  345.4 3.4 fusion.8
  348.8 2.9 copy.6
  (2 shorter events, 0.0 us)
Async XLA Ops:
  6.5 338.8 %reduce-scatter.2.cloned.1.call-start = ((), (), s32[]{:S(2)}) async-start(), calls=%async_computation.1 | async-start | bytes 18874368 | tf_op jit(solution)/shard_map/reduce_scatter | solution.py:40
Sparse Core Ops, SparseCore 0:
  64.9 280.4 reduce-scatter.1
where the time goes:
time: 359 us
  waiting for transfers between devices  279 us (78%)
  matrix products  48.9 us (14%)
  between operations  14.1 us (4%)
  blocking collectives  8.55 us (2%)
  local copies, waits for them, and re-layouts  4.88 us (1%)
    reduce_scatter x1, waiting for transfers between devices, on_device(): lax.psum_scatter(term_rows(jnp.int32(0), model_width // lax.axis_size('dp...  279 us
    dot_general x1, matrix products, term_rows(): lax.dot_general(act_block, scaled, (((0,), (0,)), ((), ())), preferred_el...  24.2 us
    dot_general x1, matrix products, ghost_partial(): jnp.einsum('etd,esd->ets', act_seq, act_seq, preferred_element_type=jnp.f...  16.9 us
    psum x1, blocking collectives, on_device(): norm_sq = lax.psum(ghost_partial(act_block, out_grads[0], examples), 'mp')  8.55 us
    dot_general x1, matrix products, ghost_partial(): jnp.einsum('etd,esd->ets', grad_seq, grad_seq, preferred_element_type=jnp...  7.76 us
  transfers between devices with their start and end apart: 1, of which 1 were waited for; matrix products, arithmetic and copies ran while one was open for 1% of the time, Pallas kernels for 0%

commit v1 on v0

--- a/solution.py
+++ b/solution.py
@@ -29,7 +29,9 @@
     batch_total = examples * lax.axis_size("dp")
     out_factor = model_width / math.sqrt(batch_total)
     act_block = acts[0]
-    norm_sq = lax.psum(ghost_partial(act_block, out_grads[0], examples), "mp")
+    norm_sq = jnp.sum(
+        lax.all_gather(ghost_partial(act_block, out_grads[0], examples), "mp"), axis=0
+    )
     scaled = scale_grads(out_grads[0], norm_sq, clip_bound[0], examples)
 
     def term_rows(begin_row, row_count, act_block=act_block, scaled=scaled):

time: 359 us -> 360 us (level)
    psum x1 -> x0, blocking collectives: 8.55 us -> none  [on_device(): norm_sq = lax.psum(ghost_partial(act_block, out_grads[0], examples), 'mp')]
    unnamed x0 -> x1, blocking collectives: none -> 8.54 us
where the time goes in v1:
time: 360 us
  waiting for transfers between devices  279 us (78%)
  matrix products  48.9 us (14%)
  between operations  14.7 us (4%)
  blocking collectives  8.54 us (2%)
  local copies, waits for them, and re-layouts  5.8 us (2%)
    reduce_scatter x1, waiting for transfers between devices, on_device(): lax.psum_scatter(term_rows(jnp.int32(0), model_width // lax.axis_size('dp...  279 us
    dot_general x1, matrix products, term_rows(): lax.dot_general(act_block, scaled, (((0,), (0,)), ((), ())), preferred_el...  24.2 us
    dot_general x1, matrix products, ghost_partial(): jnp.einsum('etd,esd->ets', act_seq, act_seq, preferred_element_type=jnp.f...  16.9 us
    unnamed x1, blocking collectives  8.54 us
    dot_general x1, matrix products, ghost_partial(): jnp.einsum('etd,esd->ets', grad_seq, grad_seq, preferred_element_type=jnp...  7.76 us
  transfers between devices with their start and end apart: 1, of which 1 were waited for; matrix products, arithmetic and copies ran while one was open for 1% of the time, Pallas kernels for 0%

profile of v1, /device:TPU:0, one launch (start us, length us, event | category | flops | bytes accessed | tf_op | source)
XLA Modules:
  0.0 360.2 jit_solution(17711162212659652402)
XLA Ops:
  6.5 0.0 reduce-scatter.2.cloned.1.call-start
  6.5 7.8 %fusion.9 = f32[4,512,512]{2,1,0:T(8,128)} fusion(bf16[4,512,1024]{2,1,0:T(8,128)(2,1)} %bitcast.30), kind=kOutput, calls=%fused_computation.11 | convolution fusion | flops 2147483648 | bytes 8388608 | tf_op jit(solution)/shard_map/etd,esd->ets/dot_general | solution.py:14
  14.3 0.0 copy-start
  14.3 16.9 %multiply_reduce_fusion = f32[4]{0:T(128)S(1)} fusion(f32[4,512,512]{2,1,0:T(8,128)} %fusion.9, bf16[4,512,4096]{2,1,0:T(8,128)(2,1)} %bitcast.29), kind=kOutput, calls=%fused_computation.6 | convolution fusion | flops 8592031744 | bytes 20971536 | tf_op jit(solution)/shard_map/etd,esd->ets/dot_general | solution.py:13
  31.2 0.0 copy-done
  31.2 0.6 dynamic-slice
  32.4 0.2 dynamic-update-slice
  32.7 8.5 %all-reduce = f32[16]{0:T(128)S(1)} all-reduce(f32[16]{0:T(128)S(1)} %dynamic-update-slice), channel_id=2, replica_groups=mesh['dp'=8,'mp'=4] {'mp'}, use_global_device_ids=true, to_apply=%add | all-reduce | flops 16 | bytes 128
  41.2 0.1 reshape.18
  42.0 0.1 broadcast_bitcast_fusion
  42.1 24.2 %fusion.2 = f32[4096,1024]{0,1:T(8,128)} fusion(bf16[1,2048,4096]{2,1,0:T(8,128)(2,1)} %param.4, bf16[1,2048,1024]{2,1,0:T(8,128)(2,1)} %param.5, f32[2048]{0:T(1024)S(1)} %bitcast.28), kind=kOutput, calls=%fused_computation.2 | convolution fusion | flops 17186160640 | bytes 37756928 | tf_op jit(solution)/shard_map/dot_general | solution.py:38
  66.3 0.0 reduce-scatter.2.cloned.1.call-update
  66.3 1.9 copy.5
  68.3 278.7 %reduce-scatter.2.cloned.1.call-done = f32[512,1024]{0,1:T(8,128)} async-done(((f32[4096,1024]{0,1:T(8,128)}), f32[512,1024]{0,1:T(8,128)}) %reduce-scatter.2.cloned.1.call-update) | async-done | bytes 2097168 | tf_op jit(solution)/shard_map/reduce_scatter | solution.py:42
  347.0 3.4 fusion.8
  350.4 2.9 copy.6
  (4 shorter events, 0.0 us)
Async XLA Ops:
  6.5 340.5 %reduce-scatter.2.cloned.1.call-start = ((), (), s32[]{:S(2)}) async-start(), calls=%async_computation.1 | async-start | bytes 18874368 | tf_op jit(solution)/shard_map/reduce_scatter | solution.py:42
  14.3 16.9 %copy-start = (u32[32]{0:T(128)S(1)}, u32[32]{0:T(128)}, u32[]{:S(2)}) copy-start(u32[32]{0:T(128)} %constant.10) | copy-start | bytes 388
Sparse Core Ops, SparseCore 0:
  66.5 280.5 reduce-scatter.1
